TPU v7x, 32 devices: a whole 2x2x4 slice. The times are simulated.
32 devices in a mesh: frame: 4 (over z), row: 8 (over y, x, core).
Axes of the slice: x: 2, y: 2, z: 4, core: 2. Of those that a mesh axis runs over, the one named last changes fastest.
Arguments:
- fine: bfloat16 [8, 320, 32, 128], P('frame', None, 'row'), may hold values from -6 to 6
- coarse: bfloat16 [4, 64, 1280], P(None, 'row', 'frame'), may hold values from -6 to 6
- w_qkv: bfloat16 [3, 1280, 1280], P(None, None, 'frame'), may hold values from -0.15625 to 0.15625
- w_out: bfloat16 [1280, 1280], P('frame'), may hold values from -0.15625 to 0.15625
- w_up: bfloat16 [1280, 320], P('frame'), may hold values from -0.15625 to 0.15625
- gain_one: float32 [320], replicated, may hold values from 0.1 to 1.9
- conv_space: bfloat16 [3, 3, 320, 320], replicated, may hold values from -0.109375 to 0.109375
- gain_two: float32 [320], replicated, may hold values from 0.1 to 1.9
- conv_time: bfloat16 [3, 320, 320], replicated, may hold values from -0.1875 to 0.1875
Outputs:
- result: bfloat16 [8, 320, 32, 128], P('frame', None, 'row')
All inputs are finite; a program needn't handle non-finite values.
Results may differ from a plain program's by a relative error of at most 0.013.
Values may be sent and summed in bfloat16 or wider, within the bound.
A program may use at most 64 MiB of HBM per device.

v0:
```python
import math
import jax
import jax.numpy as jnp
from jax import lax
from jax.sharding import PartitionSpec as P

HD = 80


def from_partner(value, axis, apart):
    mask = 2**apart
    pairs = [(source, source ^ mask) for source in range(lax.axis_size(axis))]
    return lax.ppermute(value, axis, pairs)


def with_halo(cells, sides, width):
    for axis, dim in sides:
        count = lax.axis_size(axis)
        ends = count - 1
        head = lax.slice_in_dim(cells, 0, width, axis=dim)
        tail = lax.slice_in_dim(cells, cells.shape[dim] - width, cells.shape[dim], axis=dim)
        cells = jnp.concatenate(
            [
                lax.ppermute(tail, axis, [(i, (i + 1) % count) for i in range(ends)]),
                cells,
                lax.ppermute(head, axis, [((i + 1) % count, i) for i in range(ends)]),
            ],
            axis=dim,
        )
    return cells


def norm_silu(values, gain):
    square = jnp.mean(values * values, axis=1, keepdims=True)
    scaled = values * lax.rsqrt(square + 1e-06) * gain[None, :, None, None]
    return jax.nn.silu(scaled).astype(jnp.bfloat16)


def convolve_space(extended, conv_space):
    padded = jnp.pad(extended, ((0, 0), (0, 0), (0, 0), (1, 1)))
    rows_here = extended.shape[2] - 2
    width = extended.shape[3]
    spatial = None
    for offset_y in range(3):
        for offset_x in range(3):
            window = padded[:, :, offset_y : offset_y + rows_here, offset_x : offset_x + width]
            term = jnp.einsum(
                "fcrw,cd->fdrw",
                window,
                conv_space[offset_y, offset_x],
                preferred_element_type=jnp.float32,
            )
            spatial = term if spatial is None else spatial + term
    return spatial


def local(fine, coarse, w_qkv, w_out, w_up, gain_one, conv_space, gain_two, conv_time):
    frame_count = lax.axis_size("frame")
    f_dev = fine.shape[0]
    width = fine.shape[3]
    cf_count, p_dev, c_dev = coarse.shape
    heads_local = w_qkv.shape[2] // HD
    qkv = jnp.einsum(
        "fpc,icd->ifpd",
        lax.all_gather(coarse, "frame", axis=2, tiled=True),
        w_qkv,
        preferred_element_type=jnp.float32,
    ).astype(jnp.bfloat16)
    query = qkv[0].reshape(cf_count, p_dev, heads_local, HD)
    keys = qkv[1].reshape(cf_count, p_dev, heads_local, HD)
    values = qkv[2].reshape(cf_count, p_dev, heads_local, HD)
    scores = jnp.einsum(
        "fphd,gphd->phfg", query, keys, preferred_element_type=jnp.float32
    ) / math.sqrt(HD)
    probs = jax.nn.softmax(scores, axis=-1).astype(jnp.bfloat16)
    attn = jnp.einsum("phfg,gphd->fphd", probs, values, preferred_element_type=jnp.float32).astype(
        jnp.bfloat16
    )
    attn = attn.reshape(cf_count * p_dev, heads_local * HD)
    partial_out = jnp.dot(attn, w_out, preferred_element_type=jnp.float32).reshape(
        cf_count, p_dev, -1
    )
    share = lax.psum_scatter(partial_out, "frame", scatter_dimension=2, tiled=True)
    coarse_out = (coarse.astype(jnp.float32) + share).astype(jnp.bfloat16)
    up_partial = jnp.einsum("fpc,cd->fpd", coarse_out, w_up, preferred_element_type=jnp.float32)
    up_cells = lax.psum(up_partial, "frame").astype(jnp.bfloat16)
    partner = from_partner(up_cells, "row", 0)
    is_even = lax.axis_index("row") % 2 == 0
    coarse_row = jnp.where(
        is_even,
        jnp.concatenate([up_cells, partner], axis=1),
        jnp.concatenate([partner, up_cells], axis=1),
    )
    global_frames = lax.axis_index("frame") * f_dev + jnp.arange(f_dev, dtype=jnp.int32)
    target = global_frames * cf_count // (f_dev * frame_count)
    select = (target[:, None] == jnp.arange(cf_count, dtype=jnp.int32)[None, :]).astype(jnp.float32)
    picked = jnp.einsum("tk,kwc->tcw", select, coarse_row.astype(jnp.float32))
    widened = jnp.repeat(picked, width // picked.shape[2], axis=2)
    merged = (fine.astype(jnp.float32) + widened[:, :, None, :]).astype(jnp.bfloat16)
    first = norm_silu(merged.astype(jnp.float32), gain_one)
    extended = with_halo(first, (("row", 2),), 1)
    second = norm_silu(convolve_space(extended, conv_space), gain_two)
    second_ext = with_halo(second, (("frame", 0),), 1)
    temporal = None
    for offset in range(3):
        term = jnp.einsum(
            "fcrw,cd->fdrw",
            second_ext[offset : offset + f_dev],
            conv_time[offset],
            preferred_element_type=jnp.float32,
        )
        temporal = term if temporal is None else temporal + term
    return (merged.astype(jnp.float32) + temporal).astype(jnp.bfloat16)


def solution(mesh):
    return jax.shard_map(
        local,
        mesh=mesh,
        in_specs=(
            P("frame", None, "row", None),
            P(None, "row", "frame"),
            P(None, None, "frame"),
            P("frame", None),
            P("frame", None),
            P(),
            P(),
            P(),
            P(),
        ),
        out_specs=P("frame", None, "row", None),
        check_vma=False,
    )
```

profile of v0, /device:TPU:12, one launch (start us, length us, event | category | flops | bytes accessed | tf_op | source)
XLA Modules:
  0.0 132.2 jit_solution(14206423180547574291)
XLA Ops:
  6.5 1.1 copy.53
  7.6 25.8 %all_gather.3 = bf16[4,8,1280]{1,0,2:T(4,128)(2,1)} all-gather(bf16[4,8,320]{1,0,2:T(4,128)(2,1)S(1)} %copy.53), channel_id=1, replica_groups=mesh['frame'=4,'row'=8] {'frame'}, dimensions={2}, use_global_device_ids=true | all-gather | bytes 102400 | tf_op jit(solution)/shard_map/all_gather | solution.py:65
  33.5 1.7 %copy.54 = bf16[4,8,1280]{2,1,0:T(8,128)(2,1)S(1)} copy(bf16[4,8,1280]{1,0,2:T(4,128)(2,1)} %all_gather.3) | data formatting | bytes 163840 | tf_op jit(solution)/shard_map/all_gather | solution.py:65
  35.1 0.8 fusion.34
  36.0 0.1 reshape_squeeze.10
  36.1 0.1 reshape_squeeze.11
  36.2 0.1 reshape_squeeze.9
  36.3 0.2 fusion.123
  36.5 0.4 fusion.38
  36.9 0.1 dot_general.59
  37.0 1.4 %fusion.39 = f32[4,8,1280]{2,1,0:T(8,128)S(1)} fusion(bf16[4,8,320]{2,1,0:T(8,128)(2,1)S(1)} %dot_general.59, bf16[320,1280]{1,0:T(8,128)(2,1)} %param.12), kind=kOutput, calls=%fused_computation.50 | convolution fusion | flops 26214400 | bytes 1003520 | tf_op jit(solution)/shard_map/dot_general | solution.py:80
  38.4 1.9 %copy.90 = f32[4,8,1280]{1,0,2:T(4,128)} copy(f32[4,8,1280]{2,1,0:T(8,128)S(1)} %fusion.39) | data formatting | bytes 327680
  40.4 3.3 %reshape.62 = f32[1280,32]{1,0:T(8,128)} reshape(f32[1280,4,8]{2,1,0:T(4,128)} %bitcast.157) | data formatting | bytes 327680
  43.7 21.6 %reduce-scatter.4.cloned.1.call-done = f32[320,32]{1,0:T(8,128)} async-done(((f32[1280,32]{1,0:T(8,128)}), f32[320,32]{1,0:T(8,128)}) %reduce-scatter.4.cloned.1.call-update) | async-done | bytes 40976
  65.3 2.1 %reshape.63 = f32[320,4,8]{2,1,0:T(4,128)} reshape(f32[320,32]{1,0:T(8,128)} %reduce-scatter.4.cloned.1.call-done) | data formatting | bytes 81920
  67.4 1.4 %copy.91 = f32[4,8,320]{2,1,0:T(8,128)S(1)} copy(f32[4,8,320]{1,0,2:T(4,128)} %bitcast.158) | data formatting | bytes 81920
  68.8 0.2 fusion.72
  69.0 17.1 %psum.7 = bf16[4,8,320]{2,1,0:T(8,128)(2,1)S(1)} all-reduce(f32[4,8,320]{2,1,0:T(8,128)S(1)} %fusion.72), channel_id=1, replica_groups=mesh['frame'=4,'row'=8] {'frame'}, use_global_device_ids=true, to_apply=%region_3.0 | all-reduce | flops 10240 | bytes 61440 | tf_op jit(solution)/shard_map/psum | solution.py:86
  86.1 0.1 collective-permute-start
  86.2 1.2 collective-permute-done
  87.4 0.2 convolution_bitcast_fusion
  87.6 0.8 broadcast_bitcast_fusion
  88.4 1.2 copy.62
  89.5 0.1 fusion.18
  89.7 0.5 fusion.25
  90.2 2.2 %collective-permute-start.1 = (bf16[2,320,1,128]{3,1,2,0:T(8,128)(2,1)S(1)}, bf16[2,320,1,128]{3,1,2,0:T(8,128)(2,1)S(1)}, u32[]{:S(2)}, u32[]{:S(2)}) collective-permute-start(bf16[2,320,1,128]{3,1,2,0:T(8,128)(2,1)S(1)} %get-tuple-element.7), channel_id=1, source_target_pairs={{0,1},{1,2},{2,3},{3,4},{4,5},{5,6},{6,7},{8,9},{9,10},{10,11},{11... | collective-permute-start | bytes 491528 | tf_op jit(solution)/shard_map/ppermute | solution.py:24
  92.4 4.4 %collective-permute-start.2 = (bf16[2,320,1,128]{3,1,2,0:T(8,128)(2,1)S(1)}, bf16[2,320,1,128]{3,1,2,0:T(8,128)(2,1)S(1)}, u32[]{:S(2)}, u32[]{:S(2)}) collective-permute-start(bf16[2,320,1,128]{3,1,2,0:T(8,128)(2,1)S(1)} %get-tuple-element.8), channel_id=1, source_target_pairs={{1,0},{2,1},{3,2},{4,3},{5,4},{6,5},{7,6},{9,8},{10,9},{11,10},{12... | collective-permute-start | bytes 491528 | tf_op jit(solution)/shard_map/ppermute | solution.py:26
  96.8 0.5 fusion.66
  97.4 0.5 collective-permute-done.1
  97.9 1.8 %collective-permute-done.2 = bf16[2,320,1,128]{3,1,2,0:T(8,128)(2,1)S(1)} collective-permute-done((bf16[2,320,1,128]{3,1,2,0:T(8,128)(2,1)S(1)}, bf16[2,320,1,128]{3,1,2,0:T(8,128)(2,1)S(1)}, u32[]{:S(2)}, u32[]{:S(2)}) %collective-permute-start.2) | collective-permute-done | bytes 163872 | tf_op jit(solution)/shard_map/ppermute | solution.py:26
  99.6 1.0 fusion.8
  100.6 0.5 fusion.51
  101.2 0.7 fusion.53
  101.8 0.7 fusion.44
  102.5 0.5 fusion.48
  103.0 0.5 fusion.55
  103.6 0.6 fusion.16
  104.2 0.5 fusion.46
  104.7 1.0 multiply_reduce_fusion
  105.7 0.5 fusion.29
  106.2 5.0 %collective-permute-start.4 = (bf16[1,320,4,128]{3,1,2,0:T(8,128)(2,1)S(1)}, bf16[1,320,4,128]{3,1,2,0:T(8,128)(2,1)S(1)}, u32[]{:S(2)}, u32[]{:S(2)}) collective-permute-start(bf16[1,320,4,128]{3,1,2,0:T(8,128)(2,1)S(1)} %get-tuple-element.6), channel_id=1, source_target_pairs={{8,0},{16,8},{24,16},{9,1},{17,9},{25,17},{10,2},{18,10},{26,18},{... | collective-permute-start | bytes 983048 | tf_op jit(solution)/shard_map/ppermute | solution.py:26
  111.2 1.9 %collective-permute-start.3 = (bf16[1,320,4,128]{3,1,2,0:T(8,128)(2,1)S(1)}, bf16[1,320,4,128]{3,1,2,0:T(8,128)(2,1)S(1)}, u32[]{:S(2)}, u32[]{:S(2)}) collective-permute-start(bf16[1,320,4,128]{3,1,2,0:T(8,128)(2,1)S(1)} %get-tuple-element.5), channel_id=1, source_target_pairs={{0,8},{8,16},{16,24},{1,9},{9,17},{17,25},{2,10},{10,18},{18,26},{... | collective-permute-start | bytes 983048 | tf_op jit(solution)/shard_map/ppermute | solution.py:24
  113.2 0.5 fusion.59
  113.7 5.5 %collective-permute-done.4 = bf16[1,320,4,128]{3,1,2,0:T(8,128)(2,1)S(1)} collective-permute-done((bf16[1,320,4,128]{3,1,2,0:T(8,128)(2,1)S(1)}, bf16[1,320,4,128]{3,1,2,0:T(8,128)(2,1)S(1)}, u32[]{:S(2)}, u32[]{:S(2)}) %collective-permute-start.4) | collective-permute-done | bytes 327712 | tf_op jit(solution)/shard_map/ppermute | solution.py:26
  119.2 0.5 fusion.41
  119.8 3.6 %collective-permute-done.3 = bf16[1,320,4,128]{3,1,2,0:T(8,128)(2,1)S(1)} collective-permute-done((bf16[1,320,4,128]{3,1,2,0:T(8,128)(2,1)S(1)}, bf16[1,320,4,128]{3,1,2,0:T(8,128)(2,1)S(1)}, u32[]{:S(2)}, u32[]{:S(2)}) %collective-permute-start.3) | collective-permute-done | bytes 327712 | tf_op jit(solution)/shard_map/ppermute | solution.py:24
  123.4 0.6 fusion.17
  124.0 1.3 %copy.75 = bf16[2,320,4,128]{3,2,1,0:T(4,128)(2,1)} copy(bf16[2,320,4,128]{3,1,2,0:T(8,128)(2,1)S(1)} %fusion.17) | data formatting | bytes 1310720 | tf_op jit(solution)/shard_map/convert_element_type | solution.py:113
  (27 shorter events, 0.2 us)
Async XLA Ops:
  6.5 28.6 %copy-start = (bf16[3,1280,320]{1,2,0:T(8,128)(2,1)S(1)}, bf16[3,1280,320]{1,2,0:T(8,128)(2,1)}, u32[]{:S(2)}) copy-start(bf16[3,1280,320]{1,2,0:T(8,128)(2,1)} %param.11) | copy-start | bytes 7372804
  6.5 58.8 %reduce-scatter.4.cloned.1.call-start = ((), (), s32[]{:S(2)}) async-start(), calls=%async_computation.1 | async-start | bytes 819200
  43.7 25.1 %copy-start.4 = (bf16[320,320]{1,0:T(8,128)(2,1)S(1)}, bf16[320,320]{1,0:T(8,128)(2,1)}, u32[]{:S(2)}) copy-start(bf16[320,320]{1,0:T(8,128)(2,1)} %param.13) | copy-start | bytes 614404
  43.7 25.1 %copy-start.5 = (bf16[4,8,320]{2,1,0:T(8,128)(2,1)S(1)}, bf16[4,8,320]{2,1,0:T(8,128)(2,1)}, u32[]{:S(2)}) copy-start(bf16[4,8,320]{2,1,0:T(8,128)(2,1)} %param.10) | copy-start | bytes 61444
  67.4 22.1 %copy-start.1 = (bf16[2,320,4,128]{3,2,1,0:T(4,128)(2,1)S(1)}, bf16[2,320,4,128]{3,2,1,0:T(4,128)(2,1)}, u32[]{:S(2)}) copy-start(bf16[2,320,4,128]{3,2,1,0:T(4,128)(2,1)} %param.9) | copy-start | bytes 1966084
  69.0 20.7 %copy-start.6 = (f32[320]{0:T(512)S(1)}, f32[320]{0:T(512)}, u32[]{:S(2)}) copy-start(f32[320]{0:T(512)} %param.14) | copy-start | bytes 3844
  86.1 1.3 collective-permute-start
  89.7 7.1 %copy-start.2 = (bf16[3,3,320,320]{3,2,1,0:T(8,128)(2,1)S(1)}, bf16[3,3,320,320]{3,2,1,0:T(8,128)(2,1)}, u32[]{:S(2)}) copy-start(bf16[3,3,320,320]{3,2,1,0:T(8,128)(2,1)} %param.15) | copy-start | bytes 5529604
  90.2 7.7 %collective-permute-start.1 = (bf16[2,320,1,128]{3,1,2,0:T(8,128)(2,1)S(1)}, bf16[2,320,1,128]{3,1,2,0:T(8,128)(2,1)S(1)}, u32[]{:S(2)}, u32[]{:S(2)}) collective-permute-start(bf16[2,320,1,128]{3,1,2,0:T(8,128)(2,1)S(1)} %get-tuple-element.7), channel_id=1, source_target_pairs={{0,1},{1,2},{2,3},{3,4},{4,5},{5,6},{6,7},{8,9},{9,10},{10,11},{11... | collective-permute-start | bytes 491528 | tf_op jit(solution)/shard_map/ppermute | solution.py:24
  92.4 7.2 %collective-permute-start.2 = (bf16[2,320,1,128]{3,1,2,0:T(8,128)(2,1)S(1)}, bf16[2,320,1,128]{3,1,2,0:T(8,128)(2,1)S(1)}, u32[]{:S(2)}, u32[]{:S(2)}) collective-permute-start(bf16[2,320,1,128]{3,1,2,0:T(8,128)(2,1)S(1)} %get-tuple-element.8), channel_id=1, source_target_pairs={{1,0},{2,1},{3,2},{4,3},{5,4},{6,5},{7,6},{9,8},{10,9},{11,10},{12... | collective-permute-start | bytes 491528 | tf_op jit(solution)/shard_map/ppermute | solution.py:26
  104.7 1.0 copy-start.7
  105.7 7.5 %copy-start.3 = (bf16[3,320,320]{2,1,0:T(8,128)(2,1)S(1)}, bf16[3,320,320]{2,1,0:T(8,128)(2,1)}, u32[]{:S(2)}) copy-start(bf16[3,320,320]{2,1,0:T(8,128)(2,1)} %param.17) | copy-start | bytes 1843204
  106.2 13.0 %collective-permute-start.4 = (bf16[1,320,4,128]{3,1,2,0:T(8,128)(2,1)S(1)}, bf16[1,320,4,128]{3,1,2,0:T(8,128)(2,1)S(1)}, u32[]{:S(2)}, u32[]{:S(2)}) collective-permute-start(bf16[1,320,4,128]{3,1,2,0:T(8,128)(2,1)S(1)} %get-tuple-element.6), channel_id=1, source_target_pairs={{8,0},{16,8},{24,16},{9,1},{17,9},{25,17},{10,2},{18,10},{26,18},{... | collective-permute-start | bytes 983048 | tf_op jit(solution)/shard_map/ppermute | solution.py:26
  111.2 12.1 %collective-permute-start.3 = (bf16[1,320,4,128]{3,1,2,0:T(8,128)(2,1)S(1)}, bf16[1,320,4,128]{3,1,2,0:T(8,128)(2,1)S(1)}, u32[]{:S(2)}, u32[]{:S(2)}) collective-permute-start(bf16[1,320,4,128]{3,1,2,0:T(8,128)(2,1)S(1)} %get-tuple-element.5), channel_id=1, source_target_pairs={{0,8},{8,16},{16,24},{1,9},{9,17},{17,25},{2,10},{10,18},{18,26},{... | collective-permute-start | bytes 983048 | tf_op jit(solution)/shard_map/ppermute | solution.py:24
Sparse Core Ops, SparseCore 0:
  43.8 21.4 reduce-scatter.3
where the time goes:
time: 133 us; the launch traced here: 132 us
  blocking collectives  42.9 us (32%)
  waiting for transfers between devices  34.2 us (26%)
  local copies, waits for them, and re-layouts  15.2 us (11%)
  between operations  13.7 us (10%)
  starting transfers between devices  13.6 us (10%)
  matrix products  10.4 us (8%)
  other arithmetic  2.09 us (2%)
    all_gather x1, blocking collectives, local(): lax.all_gather(coarse, 'frame', axis=2, tiled=True)  25.8 us
    unnamed x2, waiting for transfers between devices  21.7 us
    psum x1, blocking collectives, local(): up_cells = lax.psum(up_partial, 'frame').astype(jnp.bfloat16)  17.1 us
    unnamed x21, local copies, waits for them, and re-layouts  9.83 us
    ppermute x2, starting transfers between devices, with_halo(): lax.ppermute(head, axis, [((i + 1) % count, i) for i in range(ends)])  9.39 us
    ppermute x2, waiting for transfers between devices, with_halo(): lax.ppermute(head, axis, [((i + 1) % count, i) for i in range(ends)])  7.29 us
    dot_general x9, matrix products, convolve_space(): jnp.einsum('fcrw,cd->fdrw', window, conv_space[offset_y, offset_x], prefe...  5.51 us
    ppermute x2, starting transfers between devices, with_halo(): lax.ppermute(tail, axis, [(i, (i + 1) % count) for i in range(ends)])  4.12 us
  transfers between devices with their start and end apart: 6, of which 6 were waited for; matrix products, arithmetic and copies ran while one was open for 1% of the time, Pallas kernels for 0%

commit v1 on v0

--- a/solution.py
+++ b/solution.py
@@ -83,7 +83,7 @@
     share = lax.psum_scatter(partial_out, "frame", scatter_dimension=2, tiled=True)
     coarse_out = (coarse.astype(jnp.float32) + share).astype(jnp.bfloat16)
     up_partial = jnp.einsum("fpc,cd->fpd", coarse_out, w_up, preferred_element_type=jnp.float32)
-    up_cells = lax.psum(up_partial, "frame").astype(jnp.bfloat16)
+    up_cells = jnp.sum(lax.all_gather(up_partial, "frame"), axis=0).astype(jnp.bfloat16)
     partner = from_partner(up_cells, "row", 0)
     is_even = lax.axis_index("row") % 2 == 0
     coarse_row = jnp.where(

time: 133 us -> 127 us (0.955)
  blocking collectives: 42.9 us -> 40.2 us
  local copies, waits for them, and re-layouts: 15.2 us -> 13.2 us
    psum x1 -> x0, blocking collectives: 17.1 us -> none  [local(): up_cells = lax.psum(up_partial, 'frame').astype(jnp.bfloat16)]
    all_gather x0 -> x1, blocking collectives: none -> 14.4 us  [local(): lax.all_gather(up_partial, 'frame')]
    unnamed x21, local copies, waits for them, and re-layouts: 9.83 us -> 7.85 us
where the time goes in v1:
time: 127 us
  blocking collectives  40.2 us (32%)
  waiting for transfers between devices  34.2 us (27%)
  between operations  13.7 us (11%)
  local copies, waits for them, and re-layouts  13.2 us (10%)
  starting transfers between devices  12.9 us (10%)
  matrix products  10.4 us (8%)
  other arithmetic  2.11 us (2%)
    all_gather x1, blocking collectives, local(): lax.all_gather(coarse, 'frame', axis=2, tiled=True)  25.8 us
    unnamed x2, waiting for transfers between devices  21.7 us
    all_gather x1, blocking collectives, local(): lax.all_gather(up_partial, 'frame')  14.4 us
    ppermute x2, starting transfers between devices, with_halo(): lax.ppermute(head, axis, [((i + 1) % count, i) for i in range(ends)])  8.71 us
    unnamed x21, local copies, waits for them, and re-layouts  7.85 us
    ppermute x2, waiting for transfers between devices, with_halo(): lax.ppermute(head, axis, [((i + 1) % count, i) for i in range(ends)])  7.36 us
    dot_general x9, matrix products, convolve_space(): jnp.einsum('fcrw,cd->fdrw', window, conv_space[offset_y, offset_x], prefe...  5.51 us
    ppermute x2, starting transfers between devices, with_halo(): lax.ppermute(tail, axis, [(i, (i + 1) % count) for i in range(ends)])  4.12 us
  transfers between devices with their start and end apart: 6, of which 6 were waited for; matrix products, arithmetic and copies ran while one was open for 1% of the time, Pallas kernels for 0%

profile of v1, /device:TPU:12, one launch (start us, length us, event | category | flops | bytes accessed | tf_op | source)
XLA Modules:
  0.0 126.8 jit_solution(6504181350930856365)
XLA Ops:
  6.5 1.1 copy.51
  7.6 25.8 %all_gather.9 = bf16[4,8,1280]{1,0,2:T(4,128)(2,1)} all-gather(bf16[4,8,320]{1,0,2:T(4,128)(2,1)S(1)} %copy.51), channel_id=1, replica_groups=mesh['frame'=4,'row'=8] {'frame'}, dimensions={2}, use_global_device_ids=true | all-gather | bytes 102400 | tf_op jit(solution)/shard_map/all_gather | solution.py:65
  33.5 1.7 %copy.52 = bf16[4,8,1280]{2,1,0:T(8,128)(2,1)S(1)} copy(bf16[4,8,1280]{1,0,2:T(4,128)(2,1)} %all_gather.9) | data formatting | bytes 163840 | tf_op jit(solution)/shard_map/all_gather | solution.py:65
  35.1 0.8 fusion.34
  36.0 0.1 reshape_squeeze.10
  36.1 0.1 reshape_squeeze.11
  36.2 0.1 reshape_squeeze.9
  36.3 0.2 fusion.123
  36.5 0.4 fusion.38
  36.9 0.1 dot_general.59
  37.0 1.4 %fusion.39 = f32[4,8,1280]{2,1,0:T(8,128)S(1)} fusion(bf16[4,8,320]{2,1,0:T(8,128)(2,1)S(1)} %dot_general.59, bf16[320,1280]{1,0:T(8,128)(2,1)} %param.12), kind=kOutput, calls=%fused_computation.50 | convolution fusion | flops 26214400 | bytes 1003520 | tf_op jit(solution)/shard_map/dot_general | solution.py:80
  38.4 1.9 %copy.88 = f32[4,8,1280]{1,0,2:T(4,128)} copy(f32[4,8,1280]{2,1,0:T(8,128)S(1)} %fusion.39) | data formatting | bytes 327680
  40.4 3.3 %reshape.63 = f32[1280,32]{1,0:T(8,128)} reshape(f32[1280,4,8]{2,1,0:T(4,128)} %bitcast.158) | data formatting | bytes 327680
  43.7 21.6 %reduce-scatter.4.cloned.1.call-done = f32[320,32]{1,0:T(8,128)} async-done(((f32[1280,32]{1,0:T(8,128)}), f32[320,32]{1,0:T(8,128)}) %reduce-scatter.4.cloned.1.call-update) | async-done | bytes 40976
  65.3 1.2 reshape.64
  66.6 0.2 copy.89
  66.8 0.2 fusion.72
  67.0 14.4 %all-gather = f32[16,8,320]{2,1,0:T(8,128)S(1)} all-gather(f32[4,8,320]{2,1,0:T(8,128)S(1)} %fusion.72), channel_id=2, replica_groups=mesh['frame'=4,'row'=8] {'frame'}, dimensions={0}, use_global_device_ids=true | all-gather | bytes 204800 | tf_op jit(solution)/shard_map/all_gather | solution.py:86
  81.4 0.1 collective-permute-start
  81.5 1.2 collective-permute-done
  82.7 0.2 convolution_bitcast_fusion
  82.9 0.8 broadcast_bitcast_fusion
  83.7 1.2 copy.60
  84.9 0.1 fusion.18
  85.1 0.5 fusion.25
  85.6 2.2 %collective-permute-start.1 = (bf16[2,320,1,128]{3,1,2,0:T(8,128)(2,1)S(1)}, bf16[2,320,1,128]{3,1,2,0:T(8,128)(2,1)S(1)}, u32[]{:S(2)}, u32[]{:S(2)}) collective-permute-start(bf16[2,320,1,128]{3,1,2,0:T(8,128)(2,1)S(1)} %get-tuple-element.7), channel_id=1, source_target_pairs={{0,1},{1,2},{2,3},{3,4},{4,5},{5,6},{6,7},{8,9},{9,10},{10,11},{11... | collective-permute-start | bytes 491528 | tf_op jit(solution)/shard_map/ppermute | solution.py:24
  87.8 4.4 %collective-permute-start.2 = (bf16[2,320,1,128]{3,1,2,0:T(8,128)(2,1)S(1)}, bf16[2,320,1,128]{3,1,2,0:T(8,128)(2,1)S(1)}, u32[]{:S(2)}, u32[]{:S(2)}) collective-permute-start(bf16[2,320,1,128]{3,1,2,0:T(8,128)(2,1)S(1)} %get-tuple-element.8), channel_id=1, source_target_pairs={{1,0},{2,1},{3,2},{4,3},{5,4},{6,5},{7,6},{9,8},{10,9},{11,10},{12... | collective-permute-start | bytes 491528 | tf_op jit(solution)/shard_map/ppermute | solution.py:26
  92.2 0.5 fusion.66
  92.7 0.5 collective-permute-done.1
  93.2 1.8 %collective-permute-done.2 = bf16[2,320,1,128]{3,1,2,0:T(8,128)(2,1)S(1)} collective-permute-done((bf16[2,320,1,128]{3,1,2,0:T(8,128)(2,1)S(1)}, bf16[2,320,1,128]{3,1,2,0:T(8,128)(2,1)S(1)}, u32[]{:S(2)}, u32[]{:S(2)}) %collective-permute-start.2) | collective-permute-done | bytes 163872 | tf_op jit(solution)/shard_map/ppermute | solution.py:26
  95.0 1.0 fusion.8
  96.0 0.5 fusion.51
  96.5 0.7 fusion.53
  97.2 0.7 fusion.44
  97.9 0.5 fusion.48
  98.4 0.5 fusion.55
  98.9 0.6 fusion.16
  99.5 0.5 fusion.46
  100.0 1.0 multiply_reduce_fusion
  101.0 0.5 fusion.29
  101.6 4.3 %collective-permute-start.4 = (bf16[1,320,4,128]{3,1,2,0:T(8,128)(2,1)S(1)}, bf16[1,320,4,128]{3,1,2,0:T(8,128)(2,1)S(1)}, u32[]{:S(2)}, u32[]{:S(2)}) collective-permute-start(bf16[1,320,4,128]{3,1,2,0:T(8,128)(2,1)S(1)} %get-tuple-element.6), channel_id=1, source_target_pairs={{8,0},{16,8},{24,16},{9,1},{17,9},{25,17},{10,2},{18,10},{26,18},{... | collective-permute-start | bytes 983048 | tf_op jit(solution)/shard_map/ppermute | solution.py:26
  105.9 1.9 %collective-permute-start.3 = (bf16[1,320,4,128]{3,1,2,0:T(8,128)(2,1)S(1)}, bf16[1,320,4,128]{3,1,2,0:T(8,128)(2,1)S(1)}, u32[]{:S(2)}, u32[]{:S(2)}) collective-permute-start(bf16[1,320,4,128]{3,1,2,0:T(8,128)(2,1)S(1)} %get-tuple-element.5), channel_id=1, source_target_pairs={{0,8},{8,16},{16,24},{1,9},{9,17},{17,25},{2,10},{10,18},{18,26},{... | collective-permute-start | bytes 983048 | tf_op jit(solution)/shard_map/ppermute | solution.py:24
  107.8 0.5 fusion.59
  108.4 5.6 %collective-permute-done.4 = bf16[1,320,4,128]{3,1,2,0:T(8,128)(2,1)S(1)} collective-permute-done((bf16[1,320,4,128]{3,1,2,0:T(8,128)(2,1)S(1)}, bf16[1,320,4,128]{3,1,2,0:T(8,128)(2,1)S(1)}, u32[]{:S(2)}, u32[]{:S(2)}) %collective-permute-start.4) | collective-permute-done | bytes 327712 | tf_op jit(solution)/shard_map/ppermute | solution.py:26
  114.0 0.5 fusion.41
  114.5 3.5 %collective-permute-done.3 = bf16[1,320,4,128]{3,1,2,0:T(8,128)(2,1)S(1)} collective-permute-done((bf16[1,320,4,128]{3,1,2,0:T(8,128)(2,1)S(1)}, bf16[1,320,4,128]{3,1,2,0:T(8,128)(2,1)S(1)}, u32[]{:S(2)}, u32[]{:S(2)}) %collective-permute-start.3) | collective-permute-done | bytes 327712 | tf_op jit(solution)/shard_map/ppermute | solution.py:24
  118.0 0.6 fusion.17
  118.7 1.3 %copy.73 = bf16[2,320,4,128]{3,2,1,0:T(4,128)(2,1)} copy(bf16[2,320,4,128]{3,1,2,0:T(8,128)(2,1)S(1)} %fusion.17) | data formatting | bytes 1310720 | tf_op jit(solution)/shard_map/convert_element_type | solution.py:113
  (28 shorter events, 0.2 us)
Async XLA Ops:
  6.5 28.6 %copy-start = (bf16[3,1280,320]{1,2,0:T(8,128)(2,1)S(1)}, bf16[3,1280,320]{1,2,0:T(8,128)(2,1)}, u32[]{:S(2)}) copy-start(bf16[3,1280,320]{1,2,0:T(8,128)(2,1)} %param.11) | copy-start | bytes 7372804
  6.5 58.8 %reduce-scatter.4.cloned.1.call-start = ((), (), s32[]{:S(2)}) async-start(), calls=%async_computation.1 | async-start | bytes 819200
  43.7 23.2 %copy-start.4 = (bf16[320,320]{1,0:T(8,128)(2,1)S(1)}, bf16[320,320]{1,0:T(8,128)(2,1)}, u32[]{:S(2)}) copy-start(bf16[320,320]{1,0:T(8,128)(2,1)} %param.13) | copy-start | bytes 614404
  43.7 23.2 %copy-start.5 = (bf16[4,8,320]{2,1,0:T(8,128)(2,1)S(1)}, bf16[4,8,320]{2,1,0:T(8,128)(2,1)}, u32[]{:S(2)}) copy-start(bf16[4,8,320]{2,1,0:T(8,128)(2,1)} %param.10) | copy-start | bytes 61444
  66.8 18.0 %copy-start.1 = (bf16[2,320,4,128]{3,2,1,0:T(4,128)(2,1)S(1)}, bf16[2,320,4,128]{3,2,1,0:T(4,128)(2,1)}, u32[]{:S(2)}) copy-start(bf16[2,320,4,128]{3,2,1,0:T(4,128)(2,1)} %param.9) | copy-start | bytes 1966084
  81.4 3.6 %copy-start.6 = (f32[320]{0:T(512)S(1)}, f32[320]{0:T(512)}, u32[]{:S(2)}) copy-start(f32[320]{0:T(512)} %param.14) | copy-start | bytes 3844
  81.4 1.3 collective-permute-start
  85.0 7.1 %copy-start.2 = (bf16[3,3,320,320]{3,2,1,0:T(8,128)(2,1)S(1)}, bf16[3,3,320,320]{3,2,1,0:T(8,128)(2,1)}, u32[]{:S(2)}) copy-start(bf16[3,3,320,320]{3,2,1,0:T(8,128)(2,1)} %param.15) | copy-start | bytes 5529604
  85.6 7.7 %collective-permute-start.1 = (bf16[2,320,1,128]{3,1,2,0:T(8,128)(2,1)S(1)}, bf16[2,320,1,128]{3,1,2,0:T(8,128)(2,1)S(1)}, u32[]{:S(2)}, u32[]{:S(2)}) collective-permute-start(bf16[2,320,1,128]{3,1,2,0:T(8,128)(2,1)S(1)} %get-tuple-element.7), channel_id=1, source_target_pairs={{0,1},{1,2},{2,3},{3,4},{4,5},{5,6},{6,7},{8,9},{9,10},{10,11},{11... | collective-permute-start | bytes 491528 | tf_op jit(solution)/shard_map/ppermute | solution.py:24
  87.8 7.2 %collective-permute-start.2 = (bf16[2,320,1,128]{3,1,2,0:T(8,128)(2,1)S(1)}, bf16[2,320,1,128]{3,1,2,0:T(8,128)(2,1)S(1)}, u32[]{:S(2)}, u32[]{:S(2)}) collective-permute-start(bf16[2,320,1,128]{3,1,2,0:T(8,128)(2,1)S(1)} %get-tuple-element.8), channel_id=1, source_target_pairs={{1,0},{2,1},{3,2},{4,3},{5,4},{6,5},{7,6},{9,8},{10,9},{11,10},{12... | collective-permute-start | bytes 491528 | tf_op jit(solution)/shard_map/ppermute | solution.py:26
  100.0 1.0 copy-start.7
  101.0 6.8 %copy-start.3 = (bf16[3,320,320]{2,1,0:T(8,128)(2,1)S(1)}, bf16[3,320,320]{2,1,0:T(8,128)(2,1)}, u32[]{:S(2)}) copy-start(bf16[3,320,320]{2,1,0:T(8,128)(2,1)} %param.17) | copy-start | bytes 1843204
  101.6 12.4 %collective-permute-start.4 = (bf16[1,320,4,128]{3,1,2,0:T(8,128)(2,1)S(1)}, bf16[1,320,4,128]{3,1,2,0:T(8,128)(2,1)S(1)}, u32[]{:S(2)}, u32[]{:S(2)}) collective-permute-start(bf16[1,320,4,128]{3,1,2,0:T(8,128)(2,1)S(1)} %get-tuple-element.6), channel_id=1, source_target_pairs={{8,0},{16,8},{24,16},{9,1},{17,9},{25,17},{10,2},{18,10},{26,18},{... | collective-permute-start | bytes 983048 | tf_op jit(solution)/shard_map/ppermute | solution.py:26
  105.9 12.1 %collective-permute-start.3 = (bf16[1,320,4,128]{3,1,2,0:T(8,128)(2,1)S(1)}, bf16[1,320,4,128]{3,1,2,0:T(8,128)(2,1)S(1)}, u32[]{:S(2)}, u32[]{:S(2)}) collective-permute-start(bf16[1,320,4,128]{3,1,2,0:T(8,128)(2,1)S(1)} %get-tuple-element.5), channel_id=1, source_target_pairs={{0,8},{8,16},{16,24},{1,9},{9,17},{17,25},{2,10},{10,18},{18,26},{... | collective-permute-start | bytes 983048 | tf_op jit(solution)/shard_map/ppermute | solution.py:24
Sparse Core Ops, SparseCore 0:
  43.8 21.4 reduce-scatter.3
